TPU v7x, 32 devices: a whole 2x2x4 slice. The times are simulated.
32 devices in a mesh: groups: 2 (over y), users: 4 (over z), routers: 2 (over x), heads: 2 (over core).
Axes of the slice: x: 2, y: 2, z: 4, core: 2. Of those that a mesh axis runs over, the one named last changes fastest.
Arguments:
- items: bfloat16 [64, 64, 1024], P(('groups', 'users', 'routers')), parts along dimension 0, may hold values from -6 to 6
- block_owner: int32 [64, 1], P(('groups', 'users', 'routers')), parts along dimension 0, may hold values from 0 to 3; in each aligned block of 4 rows (0 to 3, 4 to 7, ...) at most 2 rows name the same one
- block_user: int32 [64], P(('groups', 'users', 'routers')), parts along dimension 0, may hold values from 0 to 1
- block_fill: int32 [64], P(('groups', 'users', 'routers')), parts along dimension 0, may hold values from 1 to 64
- prefix_keys: bfloat16 [16, 256, 1024], P(('groups', 'users'), None, 'heads'), parts along dimension 0, may hold values from -6 to 6
- prefix_values: bfloat16 [16, 256, 1024], P(('groups', 'users'), None, 'heads'), parts along dimension 0, may hold values from -6 to 6
- w_in: bfloat16 [4, 1024, 1024], P(None, 'routers', 'heads'), may hold values from -0.1875 to 0.1875
- attn_gain: bfloat16 [1024], P('heads'), may hold values from 0.25 to 1.75
- w_o: bfloat16 [1024, 1024], P('heads', 'routers'), may hold values from -0.1875 to 0.1875
- mlp_gain: bfloat16 [1024], replicated, may hold values from 0.25 to 1.75
- w_one: bfloat16 [1024, 256], replicated, may hold values from -0.1875 to 0.1875
- w_two: bfloat16 [256], replicated, may hold values from -0.375 to 0.375
Outputs:
- scores: float32 [64, 64], P(('groups', 'users', 'routers')), parts along dimension 0
There are 2 independent parts, one for each index of `groups`. A program takes and returns all parts, laid end to end along the dimension named above; an argument that names none is the same for every part. Nothing has to cross between parts.
Inputs may be any that keep to these rules, and one draw needn't show every extreme that they name: `block_owner`: within the rows of one device (aligned blocks of 4 blocks), no owner is named by more than 2 rows, and in every draw some owner is named by exactly 2 rows of some device.
All inputs are finite; a program needn't handle non-finite values.
Results may differ from a plain program's by a relative error of at most 0.005.
Values may be sent and summed in bfloat16 or wider, within the bound.
A program may use at most 64 MiB of HBM per device.

v0:
```python
import jax
import jax.numpy as jnp
from jax import lax
from jax.sharding import PartitionSpec as P

D = 1024
HEAD_DIM = 128
CAP = 2
HD = 1024
EPSILON = 1e-05


def prefix_attention(group_queries, group_users, prefix_keys, prefix_values):
    group_size, block_width, half_width = group_queries.shape
    heads_here = half_width // HEAD_DIM
    safe_user = jnp.maximum(group_users, 0)
    user_keys = jnp.take(prefix_keys, safe_user, axis=0)
    user_values = jnp.take(prefix_values, safe_user, axis=0)
    query_heads = group_queries.reshape(group_size, block_width, heads_here, HEAD_DIM)
    key_heads = user_keys.reshape(group_size, -1, heads_here, HEAD_DIM)
    value_heads = user_values.reshape(group_size, -1, heads_here, HEAD_DIM)
    raw_scores = jnp.einsum(
        "gqhd,gkhd->ghqk", query_heads, key_heads, preferred_element_type=jnp.float32
    ) * HEAD_DIM ** (-0.5)
    weights = jax.nn.silu(raw_scores).astype(jnp.bfloat16)
    summed = jnp.einsum("ghqk,gkhd->gqhd", weights, value_heads, preferred_element_type=jnp.float32)
    return summed.reshape(group_size, block_width, half_width).astype(jnp.bfloat16)


def local(
    items,
    block_owner,
    block_user,
    block_fill,
    prefix_keys,
    prefix_values,
    w_in,
    attn_gain,
    w_o,
    mlp_gain,
    w_one,
    w_two,
):
    blocks, block_width, model_width = items.shape
    row_count = blocks * block_width
    half_width = w_in.shape[2]
    heads_here = half_width // HEAD_DIM
    peer_count = lax.axis_size("users")
    slot_count = peer_count * CAP
    score_scale = HEAD_DIM ** (-0.5)
    flat_items = items.reshape(row_count, model_width)
    projected = jnp.einsum(
        "rk,pkc->prc",
        flat_items,
        lax.all_gather(w_in, "routers", axis=1, tiled=True),
        preferred_element_type=jnp.float32,
    )
    activated = jax.nn.silu(projected)
    queries = activated[0].astype(jnp.bfloat16)
    target = block_owner[:, 0]
    earlier = lax.broadcasted_iota(jnp.int32, (blocks, blocks), 1) < lax.broadcasted_iota(
        jnp.int32, (blocks, blocks), 0
    )
    same_target = target[:, None] == target[None, :]
    dest_rank = jnp.sum((same_target & earlier).astype(jnp.int32), axis=1)
    position = target * CAP + dest_rank
    selector = lax.broadcasted_iota(jnp.int32, (slot_count, blocks), 0) == position[None, :]
    block_queries = queries.reshape(blocks, block_width * half_width)
    outgoing = jnp.dot(
        selector.astype(jnp.bfloat16), block_queries, preferred_element_type=jnp.float32
    ).astype(jnp.bfloat16)
    outgoing = outgoing.reshape(peer_count, CAP, block_width, half_width)
    slot_user = jnp.sum(jnp.where(selector, block_user[None, :] + 1, 0), axis=1) - 1
    slot_user = slot_user.reshape(peer_count, CAP)
    arrived = lax.all_to_all(outgoing, "users", split_axis=0, concat_axis=0, tiled=True)
    arrived_users = lax.all_to_all(slot_user, "users", split_axis=0, concat_axis=0, tiled=True)
    sources, per_source = arrived_users.shape
    total_slots = sources * per_source
    flat_queries = arrived.reshape(total_slots, block_width, half_width)
    flat_users = arrived_users.reshape(total_slots)
    packing = jnp.argsort((flat_users < 0).astype(jnp.int32), stable=True)
    used_slots = jnp.sum((flat_users >= 0).astype(jnp.int32))
    packed_queries = jnp.take(flat_queries, packing, axis=0)
    packed_users = jnp.take(flat_users, packing, axis=0)
    needed = (used_slots + 3) // 4

    def attend_group(group_index, buffer):
        first_slot = group_index * 4
        group_queries = lax.dynamic_slice_in_dim(packed_queries, first_slot, 4, 0)
        group_users = lax.dynamic_slice_in_dim(packed_users, first_slot, 4, 0)
        result = prefix_attention(group_queries, group_users, prefix_keys, prefix_values)
        return lax.dynamic_update_slice_in_dim(buffer, result, first_slot, 0)

    packed_out = lax.fori_loop(
        0, needed, attend_group, jnp.zeros((total_slots, block_width, half_width), jnp.bfloat16)
    )
    inverse = jnp.argsort(packing)
    attended_slots = jnp.take(packed_out, inverse, axis=0)
    returned = lax.all_to_all(
        attended_slots.reshape(sources, per_source, block_width, half_width),
        "users",
        split_axis=0,
        concat_axis=0,
        tiled=True,
    )
    prefix_part = jnp.take(returned.reshape(slot_count, block_width * half_width), position, axis=0)
    prefix_part = prefix_part.reshape(row_count, heads_here, HEAD_DIM).astype(jnp.float32)
    query_heads = queries.astype(jnp.float32).reshape(row_count, heads_here, HEAD_DIM)
    self_keys = activated[1].reshape(row_count, heads_here, HEAD_DIM)
    self_values = activated[2].reshape(row_count, heads_here, HEAD_DIM)
    own_term = (
        jax.nn.silu(jnp.sum(query_heads * self_keys, axis=-1) * score_scale)[..., None]
        * self_values
    )
    attended = (prefix_part + own_term).reshape(row_count, half_width)
    totals = lax.psum((jnp.sum(attended, axis=1), jnp.sum(attended * attended, axis=1)), "heads")
    row_mean = totals[0] / HD
    row_var = totals[1] / HD - row_mean * row_mean
    gated = (
        (attended - row_mean[:, None])
        * lax.rsqrt(row_var + EPSILON)[:, None]
        * attn_gain.astype(jnp.float32)
        * activated[3]
    ).astype(jnp.bfloat16)
    partial_out = jnp.dot(
        gated,
        lax.all_gather(w_o, "routers", axis=1, tiled=True),
        preferred_element_type=jnp.float32,
    )
    mixed = lax.psum(partial_out, "heads")
    residual = flat_items.astype(jnp.float32) + mixed
    row_scale = lax.rsqrt(jnp.sum(residual * residual, axis=1) / D + EPSILON)
    normed = (residual * row_scale[:, None] * mlp_gain.astype(jnp.float32)).astype(jnp.bfloat16)
    hidden = jax.nn.silu(jnp.dot(normed, w_one, preferred_element_type=jnp.float32)).astype(
        jnp.bfloat16
    )
    block_scores = jnp.dot(hidden, w_two, preferred_element_type=jnp.float32).reshape(
        blocks, block_width
    )
    is_valid = lax.broadcasted_iota(jnp.int32, (blocks, block_width), 1) < block_fill[:, None]
    return jnp.where(is_valid, block_scores, jnp.zeros_like(block_scores))


def solution(mesh):
    placed = (
        P(("groups", "users", "routers"), None, None),
        P(("groups", "users", "routers"), None),
        P(("groups", "users", "routers")),
        P(("groups", "users", "routers")),
        P(("groups", "users"), None, "heads"),
        P(("groups", "users"), None, "heads"),
        P(None, "routers", "heads"),
        P("heads"),
        P("heads", "routers"),
        P(),
        P(),
        P(),
    )
    return jax.shard_map(
        local,
        mesh=mesh,
        in_specs=placed,
        out_specs=P(("groups", "users", "routers"), None),
        check_vma=False,
    )
```

profile of v0, /device:TPU:0, one launch (start us, length us, event | category | flops | bytes accessed | tf_op | source)
XLA Modules:
  0.0 166.5 jit_solution(10524344665358077682)
XLA Ops:
  6.5 4.2 %copy.36 = bf16[4,512,512]{1,2,0:T(8,128)(2,1)} copy(bf16[4,512,512]{2,1,0:T(8,128)(2,1)} %param.24) | data formatting | bytes 4194304 | tf_op args[6]
  10.8 0.6 copy-done.10
  11.4 0.2 convert_reduce_fusion
  11.6 0.1 select_reduce_fusion
  11.7 0.7 sub.21
  12.4 6.3 %all-to-all-start = ((s32[4,1,2]{2,1,0:T(1,128)}), s32[4,1,2]{2,1,0:T(1,128)S(1)}, u32[]{:S(2)}, u32[]{:S(2)}) async-start(s32[4,1,2]{2,1,0:T(1,128)} %bitcast.5), calls=%async_computation | async-start | bytes 4096 | tf_op jit(solution)/shard_map/all_to_all | solution.py:76
  18.7 0.7 all-gather.5.cloned.1.call-update
  19.4 4.8 %all-to-all-done = s32[4,1,2]{2,1,0:T(1,128)S(1)} async-done(((s32[4,1,2]{2,1,0:T(1,128)}), s32[4,1,2]{2,1,0:T(1,128)S(1)}, u32[]{:S(2)}, u32[]{:S(2)}) %all-to-all-start) | async-done | bytes 64 | tf_op jit(solution)/shard_map/all_to_all | solution.py:76
  24.2 0.5 broadcast.235
  24.7 1.3 fusion.40
  26.1 1.0 sort.34
  27.1 43.4 %all-gather.3.cloned.1.call-done = bf16[4,1024,512]{1,2,0:T(8,128)(2,1)} async-done(((bf16[4,512,512]{1,2,0:T(8,128)(2,1)}), bf16[4,1024,512]{1,2,0:T(8,128)(2,1)}) %all-gather.3.cloned.1.call-update) | async-done | bytes 4194320 | tf_op jit(solution)/shard_map/all_gather | solution.py:55
  70.4 3.6 %bitcast_multiply_fusion = f32[4,256,512]{1,2,0:T(8,128)S(1)} fusion(bf16[4,1024,512]{1,2,0:T(8,128)(2,1)} %all-gather.3.cloned.1.call-done, bf16[256,1024,1]{1,0,2:T(8,128)(2,1)S(1)} %bitcast.106), kind=kOutput, calls=%fused_computation.28 | convolution fusion | flops 1075838976 | bytes 6815744 | tf_op jit(solution)/shard_map/rk,pkc->prc/dot_general | solution.py:52
  74.0 1.3 copy-done.5
  75.4 0.9 slice_multiply_fusion
  76.3 0.1 copy.37
  76.4 0.2 convert_element_type.76
  76.6 0.4 convolution_convert_fusion.1
  77.0 1.0 copy.43
  78.0 4.7 %all-to-all-start.1 = ((bf16[4,2,64,512]{3,2,1,0:T(8,128)(2,1)}), bf16[4,2,64,512]{3,2,1,0:T(8,128)(2,1)S(1)}, u32[]{:S(2)}, u32[]{:S(2)}) async-start(bf16[4,2,64,512]{3,2,1,0:T(8,128)(2,1)} %bitcast.27), calls=%async_computation.1 | async-start | bytes 1048576 | tf_op jit(solution)/shard_map/all_to_all | solution.py:75
  83.4 0.6 gather_fusion.2
  84.0 1.0 sort.35
  85.0 12.0 %all-to-all-done.1 = bf16[4,2,64,512]{3,2,1,0:T(8,128)(2,1)S(1)} async-done(((bf16[4,2,64,512]{3,2,1,0:T(8,128)(2,1)}), bf16[4,2,64,512]{3,2,1,0:T(8,128)(2,1)S(1)}, u32[]{:S(2)}, u32[]{:S(2)}) %all-to-all-start.1) | async-done | bytes 524320 | tf_op jit(solution)/shard_map/all_to_all | solution.py:75
  97.0 0.6 gather_fusion.4
  97.6 0.9 broadcast_select_fusion.1
  98.6 0.9 broadcast_in_dim.66
  99.4 6.1 %while.10 = (s32[]{:T(128)}, bf16[8,64,512]{2,1,0:T(8,128)(2,1)}, s32[]{:T(128)}, s32[8]{0:T(128)S(1)}, bf16[2,256,512]{2,1,0:T(8,128)(2,1)S(1)}, /*index=5*/bf1...) while((s32[]{:T(128)}, bf16[8,64,512]{2,1,0:T(8,128)(2,1)}, ...), condition=%wide.region_5.8_spmd, body=%wide.region_4.7_spmd.sunk | while | flops 136971280 | bytes 13635875 | solution.py:94
  99.5 0.6 gather_fusion
  100.1 0.6 gather_fusion.1
  100.7 1.5 select_bitcast_fusion.3
  102.3 2.5 %fusion.55 = bf16[4,4,8,8,128]{4,3,2,1,0:T(8,128)(2,1)S(1)} fusion(bf16[4,32,4,8,128]{4,3,2,1,0:T(8,128)(2,1)} %get-tuple-element.135, bf16[4,32,4,8,128]{4,3,2,1,0:T(8,128)(2,1)} %get-tuple-element.136, bf16[8,64,512]{2,1,0:T(8,128)(2,1)} %get-tuple-element.164, s32[]{:T(128)S(6)} %select_n.93), kind=kOutput, calls=%fused_computation.8.clone.1 | convolution fusion | flops 135921664 | bytes 2621444 | tf_op jit(solution)/shard_map/while/body/ghqk,gkhd->gqhd/dot_general | solution.py:26
  104.8 0.7 bitcast_dynamic-update-slice_fusion.2
  105.5 1.7 %gather_fusion.5 = bf16[8,64,512]{2,1,0:T(8,128)(2,1)S(1)} fusion(bf16[8,64,512]{2,1,0:T(8,128)(2,1)} %get-tuple-element.174, s32[1024]{0:T(1024)S(1)} %pad_clamp_fusion.2), kind=kCustom, calls=%fused_computation.2.clone | custom fusion | bytes 1048608 | tf_op jit(solution)/shard_map/jit(_take)/gather | solution.py:98
  107.2 0.9 broadcast_select_fusion
  108.1 3.5 %all-to-all-start.2 = ((bf16[4,2,64,512]{3,2,1,0:T(8,128)(2,1)}), bf16[4,2,64,512]{3,2,1,0:T(8,128)(2,1)S(1)}, u32[]{:S(2)}, u32[]{:S(2)}) async-start(bf16[4,2,64,512]{3,2,1,0:T(8,128)(2,1)} %bitcast.9), calls=%async_computation.2 | async-start | bytes 1048576 | tf_op jit(solution)/shard_map/all_to_all | solution.py:99
  111.9 13.7 %all-to-all-done.2 = bf16[4,2,64,512]{3,2,1,0:T(8,128)(2,1)S(1)} async-done(((bf16[4,2,64,512]{3,2,1,0:T(8,128)(2,1)}), bf16[4,2,64,512]{3,2,1,0:T(8,128)(2,1)S(1)}, u32[]{:S(2)}, u32[]{:S(2)}) %all-to-all-start.2) | async-done | bytes 524320 | tf_op jit(solution)/shard_map/all_to_all | solution.py:99
  125.6 0.3 copy.44
  125.9 0.8 gather_fusion.3
  126.7 0.2 gather.18
  126.9 0.1 copy.38
  127.1 0.5 copy-done.6
  127.5 0.1 fusion.39
  127.7 2.5 %all-reduce = (f32[256]{0:T(256)S(1)}, f32[256]{0:T(256)S(1)}) all-reduce(f32[256]{0:T(256)S(1)} %get-tuple-element.51, f32[256]{0:T(256)S(1)} %get-tuple-element.50), channel_id=1, replica_groups=mesh['groups'=2,'users'=4,'routers'=2,'heads'=2] {'heads'}, use_global_device_ids=true, to_apply=%region_11.14 | all-reduce | flops 512 | bytes 4096 | tf_op jit(solution)/shard_map/psum | solution.py:116
  130.2 2.8 %fusion.27 = f32[256,1024]{1,0:T(8,128)} fusion(bf16[512,1024]{1,0:T(8,128)(2,1)} %all-gather.5.cloned.1.call-done, f32[4,256,512]{1,2,0:T(8,128)S(1)} %copy-done.6, f32[256,512]{0,1:T(8,128)S(1)} %get-tuple-element.72, f32[512]{0:T(512)S(1)} %convert_element_type.80, f32[256]{0:T(256)S(1)} %get-tuple-element.82, f32[256]{0:T(256)S(1)} %get-tuple-element.81), kind=kOutput, calls=%fused_computation.50 | convolution fusion | flops 269090816 | bytes 3149824 | tf_op jit(solution)/shard_map/dot_general | solution.py:125
  133.1 22.9 %all-reduce.3.cloned.1.call-done = f32[256,1024]{1,0:T(8,128)} async-done(((f32[256,1024]{1,0:T(8,128)}), f32[256,1024]{1,0:T(8,128)}) %all-reduce.3.cloned.1.call-update) | async-done | bytes 1048592 | tf_op jit(solution)/shard_map/psum | solution.py:130
  155.9 1.6 multiply_reduce_fusion
  157.5 1.7 %fusion.29 = f32[1,256]{1,0:T(1,128)S(1)} fusion(bf16[256,1]{0,1:T(2,128)(2,1)S(1)} %reshape.186, bf16[1024,256]{1,0:T(8,128)(2,1)S(1)} %copy-done, f32[256,1024]{1,0:T(8,128)} %all-reduce.3.cloned.1.call-done, bf16[256,1024]{1,0:T(8,128)(2,1)S(1)} %bitcast.107, f32[1024]{0:T(1024)S(1)} %convert_element_type.82, f32[256]{0:T(256)S(1)} %add_rsqrt_fusion), kind=kOutput, calls=%fused_computation.52 | convolution fusion | flops 135987200 | bytes 2103808 | tf_op jit(solution)/shard_map/dot_general | solution.py:137
  159.3 0.7 fusion.35
  (59 shorter events, 0.7 us)
Async XLA Ops:
  6.5 151.0 %copy-start = (bf16[1024,256]{1,0:T(8,128)(2,1)S(1)}, bf16[1024,256]{1,0:T(8,128)(2,1)}, u32[]{:S(2)}) copy-start(bf16[1024,256]{1,0:T(8,128)(2,1)} %param.28) | copy-start | bytes 1572868
  6.5 63.9 %all-gather.3.cloned.1.call-start = ((), (), s32[]{:S(2)}) async-start(), calls=%async_computation.3 | async-start | bytes 6291456 | tf_op jit(solution)/shard_map/all_gather | solution.py:55
  10.7 0.7 copy-start.10
  10.7 0.8 copy-start.12
  10.8 59.7 %copy-start.7 = (bf16[4,64,1024]{2,1,0:T(8,128)(2,1)S(1)}, bf16[4,64,1024]{2,1,0:T(8,128)(2,1)}, u32[]{:S(2)}) copy-start(bf16[4,64,1024]{2,1,0:T(8,128)(2,1)} %param.18) | copy-start | bytes 1572868
  12.4 11.8 %all-to-all-start = ((s32[4,1,2]{2,1,0:T(1,128)}), s32[4,1,2]{2,1,0:T(1,128)S(1)}, u32[]{:S(2)}, u32[]{:S(2)}) async-start(s32[4,1,2]{2,1,0:T(1,128)} %bitcast.5), calls=%async_computation | async-start | bytes 4096 | tf_op jit(solution)/shard_map/all_to_all | solution.py:76
  18.7 111.4 %all-gather.5.cloned.1.call-start = ((), (), s32[]{:S(2)}) async-start(), calls=%async_computation.4 | async-start | bytes 1572864 | tf_op jit(solution)/shard_map/all_gather | solution.py:127
  74.0 1.4 copy-start.5
  78.0 21.4 %copy-start.1 = (bf16[2,256,512]{2,1,0:T(8,128)(2,1)S(1)}, bf16[2,256,512]{2,1,0:T(8,128)(2,1)}, u32[]{:S(2)}) copy-start(bf16[2,256,512]{2,1,0:T(8,128)(2,1)} %param.23) | copy-start | bytes 1572868
  78.0 21.4 %copy-start.2 = (bf16[2,256,512]{2,1,0:T(8,128)(2,1)S(1)}, bf16[2,256,512]{2,1,0:T(8,128)(2,1)}, u32[]{:S(2)}) copy-start(bf16[2,256,512]{2,1,0:T(8,128)(2,1)} %param.22) | copy-start | bytes 1572868
  78.0 19.1 %all-to-all-start.1 = ((bf16[4,2,64,512]{3,2,1,0:T(8,128)(2,1)}), bf16[4,2,64,512]{3,2,1,0:T(8,128)(2,1)S(1)}, u32[]{:S(2)}, u32[]{:S(2)}) async-start(bf16[4,2,64,512]{3,2,1,0:T(8,128)(2,1)} %bitcast.27), calls=%async_computation.1 | async-start | bytes 1048576 | tf_op jit(solution)/shard_map/all_to_all | solution.py:75
  102.3 3.2 %copy-start.3 = (bf16[2,256,512]{2,1,0:T(8,128)(2,1)S(1)}, bf16[2,256,512]{2,1,0:T(8,128)(2,1)}, u32[]{:S(2)}) copy-start(bf16[2,256,512]{2,1,0:T(8,128)(2,1)} %get-tuple-element.184) | copy-start | bytes 1572868 | tf_op jit(solution)/shard_map/while
  105.5 6.3 %copy-start.11 = (bf16[512]{0:T(512)(128)(2,1)S(1)}, bf16[512]{0:T(512)(128)(2,1)}, u32[]{:S(2)}) copy-start(bf16[512]{0:T(512)(128)(2,1)} %param.25) | copy-start | bytes 3076
  105.5 6.3 %copy-start.4 = (f32[1,256,512]{1,2,0:T(8,128)S(1)}, f32[1,256,512]{1,2,0:T(8,128)}, u32[]{:S(2)}) copy-start(f32[1,256,512]{1,2,0:T(8,128)} %get-tuple-element.77) | copy-start | bytes 1572868
  108.1 17.5 %all-to-all-start.2 = ((bf16[4,2,64,512]{3,2,1,0:T(8,128)(2,1)}), bf16[4,2,64,512]{3,2,1,0:T(8,128)(2,1)S(1)}, u32[]{:S(2)}, u32[]{:S(2)}) async-start(bf16[4,2,64,512]{3,2,1,0:T(8,128)(2,1)} %bitcast.9), calls=%async_computation.2 | async-start | bytes 1048576 | tf_op jit(solution)/shard_map/all_to_all | solution.py:99
  111.6 44.3 %all-reduce.3.cloned.1.call-start = ((), (), s32[]{:S(2)}) async-start(), calls=%async_computation.5 | async-start | bytes 2097152 | tf_op jit(solution)/shard_map/psum | solution.py:130
  125.9 1.6 copy-start.6
  130.2 2.8 %copy-start.9 = (bf16[1024]{0:T(1024)(128)(2,1)S(1)}, bf16[1024]{0:T(1024)(128)(2,1)}, u32[]{:S(2)}) copy-start(bf16[1024]{0:T(1024)(128)(2,1)} %param.27) | copy-start | bytes 6148
  130.2 2.9 %copy-start.14 = (bf16[256]{0:T(256)(128)(2,1)S(1)}, bf16[256]{0:T(256)(128)(2,1)}, u32[]{:S(2)}) copy-start(bf16[256]{0:T(256)(128)(2,1)} %param.29) | copy-start | bytes 1540
  133.0 24.5 %copy-start.8 = (bf16[4,64,1024]{2,1,0:T(8,128)(2,1)S(1)}, bf16[4,64,1024]{2,1,0:T(8,128)(2,1)}, u32[]{:S(2)}) copy-start(bf16[4,64,1024]{2,1,0:T(8,128)(2,1)} %param.18) | copy-start | bytes 1572868
  133.0 26.3 %copy-start.13 = (s32[4]{0:T(128)S(1)}, s32[4]{0:T(128)}, u32[]{:S(2)}) copy-start(s32[4]{0:T(128)} %param.21) | copy-start | bytes 52
Sparse Core Ops, SparseCore 0:
  10.9 59.4 all-gather.2
  72.0 21.2 all-gather.4
  133.1 22.7 all-reduce.2
where the time goes:
time: 167 us; the launch traced here: 166 us
  waiting for transfers between devices  97.4 us (58%)
  local copies, waits for them, and re-layouts  16.6 us (10%)
  starting transfers between devices  14.6 us (9%)
  between operations  14 us (8%)
  matrix products  11 us (7%)
  other arithmetic  10.4 us (6%)
  blocking collectives  2.46 us (1%)
    all_gather x1, waiting for transfers between devices, local(): lax.all_gather(w_in, 'routers', axis=1, tiled=True)  43.4 us
    psum x1, waiting for transfers between devices, local(): mixed = lax.psum(partial_out, 'heads')  22.9 us
    all_to_all x1, waiting for transfers between devices, local(): lax.all_to_all(attended_slots.reshape(sources, per_source, block_width, h...  13.7 us
    all_to_all x1, waiting for transfers between devices, local(): lax.all_to_all(outgoing, 'users', split_axis=0, concat_axis=0, tiled=True)  12 us
    unnamed x32, local copies, waits for them, and re-layouts  7.95 us
    all_to_all x1, starting transfers between devices, local(): lax.all_to_all(slot_user, 'users', split_axis=0, concat_axis=0, tiled=True)  6.35 us
    all_to_all x1, waiting for transfers between devices, local(): lax.all_to_all(slot_user, 'users', split_axis=0, concat_axis=0, tiled=True)  4.76 us
    all_to_all x1, starting transfers between devices, local(): lax.all_to_all(outgoing, 'users', split_axis=0, concat_axis=0, tiled=True)  4.73 us
  transfers between devices with their start and end apart: 6, of which 5 were waited for; matrix products, arithmetic and copies ran while one was open for 15% of the time, Pallas kernels for 0%

commit v1 on v0

--- a/solution.py
+++ b/solution.py
@@ -49,12 +49,27 @@
     slot_count = peer_count * CAP
     score_scale = HEAD_DIM ** (-0.5)
     flat_items = items.reshape(row_count, model_width)
-    projected = jnp.einsum(
+    devices, index = (lax.axis_size("routers"), lax.axis_index("routers"))
+    behind = [(i, (i - 1) % devices) for i in range(devices)]
+    width = w_in.shape[1]
+    held = w_in
+    running = jnp.einsum(
         "rk,pkc->prc",
-        flat_items,
-        lax.all_gather(w_in, "routers", axis=1, tiled=True),
+        lax.dynamic_slice_in_dim(flat_items, index * width, held.shape[1], axis=1),
+        held,
         preferred_element_type=jnp.float32,
     )
+    for step in range(1, devices):
+        held = lax.ppermute(held, "routers", behind)
+        running = running + jnp.einsum(
+            "rk,pkc->prc",
+            lax.dynamic_slice_in_dim(
+                flat_items, (index + step) % devices * width, held.shape[1], axis=1
+            ),
+            held,
+            preferred_element_type=jnp.float32,
+        )
+    projected = running
     activated = jax.nn.silu(projected)
     queries = activated[0].astype(jnp.bfloat16)
     target = block_owner[:, 0]

time: 167 us -> 159 us (0.952)
  waiting for transfers between devices: 97.4 us -> 87.3 us
  local copies, waits for them, and re-layouts: 16.6 us -> 13.4 us
  starting transfers between devices: 14.6 us -> 16.6 us
  other arithmetic: 10.4 us -> 12.3 us
    all_gather x1 -> x0, waiting for transfers between devices: 43.4 us -> none  [local(): lax.all_gather(w_in, 'routers', axis=1, tiled=True)]
    ppermute x0 -> x1, waiting for transfers between devices: none -> 30.4 us  [local(): held = lax.ppermute(held, 'routers', behind)]
    all_gather x1, waiting for transfers between devices: 0.01 us -> 10.1 us  [local(): lax.all_gather(w_o, 'routers', axis=1, tiled=True)]
    unnamed x32 -> x29, local copies, waits for them, and re-layouts: 7.95 us -> 2.64 us
    psum x1, waiting for transfers between devices: 22.9 us -> 19.5 us  [local(): mixed = lax.psum(partial_out, 'heads')]
    ppermute x0 -> x1, starting transfers between devices: none -> 2.97 us  [local(): held = lax.ppermute(held, 'routers', behind)]
    all_to_all x1, waiting for transfers between devices: 4.76 us -> 3.05 us  [local(): lax.all_to_all(slot_user, 'users', split_axis=0, concat_axis=0, tiled=True)]
    dot_general x1 -> x2, matrix products: 3.6 us -> 4.87 us  [the longest x1 2.44 us: local(): jnp.einsum('rk,pkc->prc', lax.dynamic_slice_in_dim(flat_items, (index + s...]
  transfers between devices with their start and end apart: 6 -> 6, of which waited for: 5 -> 6; matrix products, arithmetic and copies ran while one was open for 15% -> 9% of each run, Pallas kernels for 0% -> 0%
where the time goes in v1:
time: 159 us
  waiting for transfers between devices  87.3 us (55%)
  starting transfers between devices  16.6 us (10%)
  between operations  14.3 us (9%)
  local copies, waits for them, and re-layouts  13.4 us (8%)
  other arithmetic  12.3 us (8%)
  matrix products  12.2 us (8%)
  blocking collectives  2.47 us (2%)
    ppermute x1, waiting for transfers between devices, local(): held = lax.ppermute(held, 'routers', behind)  30.4 us
    psum x1, waiting for transfers between devices, local(): mixed = lax.psum(partial_out, 'heads')  19.5 us
    all_to_all x1, waiting for transfers between devices, local(): lax.all_to_all(attended_slots.reshape(sources, per_source, block_width, h...  12.2 us
    all_to_all x1, waiting for transfers between devices, local(): lax.all_to_all(outgoing, 'users', split_axis=0, concat_axis=0, tiled=True)  11.3 us
    all_gather x1, waiting for transfers between devices, local(): lax.all_gather(w_o, 'routers', axis=1, tiled=True)  10.1 us
    all_to_all x1, starting transfers between devices, local(): lax.all_to_all(outgoing, 'users', split_axis=0, concat_axis=0, tiled=True)  5.25 us
    all_to_all x1, starting transfers between devices, local(): lax.all_to_all(slot_user, 'users', split_axis=0, concat_axis=0, tiled=True)  4.87 us
    all_to_all x1, starting transfers between devices, local(): lax.all_to_all(attended_slots.reshape(sources, per_source, block_width, h...  3.47 us
  transfers between devices with their start and end apart: 6, of which 6 were waited for; matrix products, arithmetic and copies ran while one was open for 9% of the time, Pallas kernels for 0%

profile of v1, /device:TPU:0, one launch (start us, length us, event | category | flops | bytes accessed | tf_op | source)
XLA Modules:
  0.0 158.7 jit_solution(14207532608884626713)
XLA Ops:
  6.5 3.0 %collective-permute-start = (bf16[4,512,512]{2,1,0:T(8,128)(2,1)}, bf16[4,512,512]{2,1,0:T(8,128)(2,1)}, u32[]{:S(2)}, u32[]{:S(2)}) collective-permute-start(bf16[4,512,512]{2,1,0:T(8,128)(2,1)} %param.24), channel_id=1, source_target_pairs={{0,2},{2,0},{1,3},{3,1},{4,6},{6,4},{5,7},{7,5},{8,10},{10,8},{9,1... | collective-permute-start | bytes 6291464 | tf_op jit(solution)/shard_map/ppermute | solution.py:63
  9.5 0.9 convert_reduce_fusion
  10.4 0.7 multiply_add_fusion
  11.2 0.7 sub.21
  11.9 4.9 %all-to-all-start = ((s32[4,1,2]{2,1,0:T(1,128)}), s32[4,1,2]{2,1,0:T(1,128)S(1)}, u32[]{:S(2)}, u32[]{:S(2)}) async-start(s32[4,1,2]{2,1,0:T(1,128)} %bitcast.5), calls=%async_computation | async-start | bytes 4096 | tf_op jit(solution)/shard_map/all_to_all | solution.py:91
  16.7 2.4 %fusion.29 = f32[256,4,512]{2,0,1:T(8,128)S(1)} fusion(bf16[4,512,512]{2,1,0:T(8,128)(2,1)} %param.24, bf16[256,1024]{1,0:T(8,128)(2,1)} %bitcast.110, s32[]{:T(128)S(6)} %select_n.70), kind=kOutput, calls=%fused_computation.52 | convolution fusion | flops 536870912 | bytes 4456452 | tf_op jit(solution)/shard_map/rk,pkc->prc/dot_general | solution.py:56
  19.2 3.1 %all-to-all-done = s32[4,1,2]{2,1,0:T(1,128)S(1)} async-done(((s32[4,1,2]{2,1,0:T(1,128)}), s32[4,1,2]{2,1,0:T(1,128)S(1)}, u32[]{:S(2)}, u32[]{:S(2)}) %all-to-all-start) | async-done | bytes 64 | tf_op jit(solution)/shard_map/all_to_all | solution.py:91
  22.2 0.5 broadcast.236
  22.7 1.3 fusion.46
  24.1 1.0 sort.34
  25.1 30.4 %collective-permute-done = bf16[4,512,512]{2,1,0:T(8,128)(2,1)} collective-permute-done((bf16[4,512,512]{2,1,0:T(8,128)(2,1)}, bf16[4,512,512]{2,1,0:T(8,128)(2,1)}, u32[]{:S(2)}, u32[]{:S(2)}) %collective-permute-start) | collective-permute-done | bytes 2097184 | tf_op jit(solution)/shard_map/ppermute | solution.py:63
  55.4 2.4 %bitcast_multiply_fusion = f32[4,256,512]{2,1,0:T(8,128)S(1)} fusion(f32[256,4,512]{2,0,1:T(8,128)S(1)} %fusion.29, bf16[4,512,512]{2,1,0:T(8,128)(2,1)} %collective-permute-done, bf16[256,1024]{1,0:T(8,128)(2,1)S(1)} %bitcast.111, s32[]{:T(128)S(6)} %select_n.72), kind=kOutput, calls=%fused_computation.28 | convolution fusion | flops 539492352 | bytes 6553604 | tf_op jit(solution)/shard_map/rk,pkc->prc/dot_general | solution.py:64
  57.9 1.3 copy-done.5
  59.2 0.9 slice_multiply_fusion
  60.1 0.2 convert_element_type.76
  60.3 0.4 convolution_convert_fusion.1
  60.7 1.0 copy.46
  61.7 5.3 %all-to-all-start.1 = ((bf16[4,2,64,512]{3,2,1,0:T(8,128)(2,1)}), bf16[4,2,64,512]{3,2,1,0:T(8,128)(2,1)S(1)}, u32[]{:S(2)}, u32[]{:S(2)}) async-start(bf16[4,2,64,512]{3,2,1,0:T(8,128)(2,1)} %bitcast.25), calls=%async_computation.1 | async-start | bytes 1048576 | tf_op jit(solution)/shard_map/all_to_all | solution.py:90
  67.6 0.6 gather_fusion.2
  68.3 1.0 sort.35
  69.3 11.3 %all-to-all-done.1 = bf16[4,2,64,512]{3,2,1,0:T(8,128)(2,1)S(1)} async-done(((bf16[4,2,64,512]{3,2,1,0:T(8,128)(2,1)}), bf16[4,2,64,512]{3,2,1,0:T(8,128)(2,1)S(1)}, u32[]{:S(2)}, u32[]{:S(2)}) %all-to-all-start.1) | async-done | bytes 524320 | tf_op jit(solution)/shard_map/all_to_all | solution.py:90
  80.6 0.6 gather_fusion.4
  81.2 0.9 broadcast_select_fusion.1
  82.1 0.9 broadcast_in_dim.66
  83.0 6.1 %while.10 = (s32[]{:T(128)}, bf16[8,64,512]{2,1,0:T(8,128)(2,1)}, s32[]{:T(128)}, s32[8]{0:T(128)S(1)}, bf16[2,256,512]{2,1,0:T(8,128)(2,1)S(1)}, /*index=5*/bf1...) while((s32[]{:T(128)}, bf16[8,64,512]{2,1,0:T(8,128)(2,1)}, ...), condition=%wide.region_5.8_spmd, body=%wide.region_4.7_spmd.sunk | while | flops 136971280 | bytes 13635875 | solution.py:109
  83.1 0.6 gather_fusion
  83.7 0.6 gather_fusion.1
  84.3 1.5 select_bitcast_fusion.3
  85.8 2.5 %fusion.61 = bf16[4,4,8,8,128]{4,3,2,1,0:T(8,128)(2,1)S(1)} fusion(bf16[4,32,4,8,128]{4,3,2,1,0:T(8,128)(2,1)} %get-tuple-element.135, bf16[4,32,4,8,128]{4,3,2,1,0:T(8,128)(2,1)} %get-tuple-element.136, bf16[8,64,512]{2,1,0:T(8,128)(2,1)} %get-tuple-element.164, s32[]{:T(128)S(6)} %select_n.108), kind=kOutput, calls=%fused_computation.8.clone.1 | convolution fusion | flops 135921664 | bytes 2621444 | tf_op jit(solution)/shard_map/while/body/ghqk,gkhd->gqhd/dot_general | solution.py:26
  88.3 0.7 bitcast_dynamic-update-slice_fusion.2
  89.1 1.7 %gather_fusion.5 = bf16[8,64,512]{2,1,0:T(8,128)(2,1)S(1)} fusion(bf16[8,64,512]{2,1,0:T(8,128)(2,1)} %get-tuple-element.173, s32[1024]{0:T(1024)S(1)} %pad_clamp_fusion.2), kind=kCustom, calls=%fused_computation.2.clone | custom fusion | bytes 1048608 | tf_op jit(solution)/shard_map/jit(_take)/gather | solution.py:113
  90.8 0.9 broadcast_select_fusion
  91.7 3.5 %all-to-all-start.2 = ((bf16[4,2,64,512]{3,2,1,0:T(8,128)(2,1)}), bf16[4,2,64,512]{3,2,1,0:T(8,128)(2,1)S(1)}, u32[]{:S(2)}, u32[]{:S(2)}) async-start(bf16[4,2,64,512]{3,2,1,0:T(8,128)(2,1)} %bitcast.10), calls=%async_computation.2 | async-start | bytes 1048576 | tf_op jit(solution)/shard_map/all_to_all | solution.py:114
  95.2 0.7 all-gather.2.cloned.1.call-update
  96.3 0.3 reduce_sum.69
  96.9 12.2 %all-to-all-done.2 = bf16[4,2,64,512]{3,2,1,0:T(8,128)(2,1)S(1)} async-done(((bf16[4,2,64,512]{3,2,1,0:T(8,128)(2,1)}), bf16[4,2,64,512]{3,2,1,0:T(8,128)(2,1)S(1)}, u32[]{:S(2)}, u32[]{:S(2)}) %all-to-all-start.2) | async-done | bytes 524320 | tf_op jit(solution)/shard_map/all_to_all | solution.py:114
  109.2 0.3 copy.47
  109.5 1.5 gather_fusion.3
  111.0 1.1 gather.18
  112.1 0.3 mul.128
  112.5 0.3 fusion.45
  112.8 2.5 %all-reduce = (f32[256]{0:T(256)S(1)}, f32[256]{0:T(256)S(1)}) all-reduce(f32[256]{0:T(256)S(1)} %get-tuple-element.51, f32[256]{0:T(256)S(1)} %get-tuple-element.50), channel_id=1, replica_groups=mesh['groups'=2,'users'=4,'routers'=2,'heads'=2] {'heads'}, use_global_device_ids=true, to_apply=%region_11.14 | all-reduce | flops 512 | bytes 4096 | tf_op jit(solution)/shard_map/psum | solution.py:131
  115.3 10.1 %all-gather.2.cloned.1.call-done = bf16[512,1024]{1,0:T(8,128)(2,1)} async-done(((bf16[512,512]{1,0:T(8,128)(2,1)}), bf16[512,1024]{1,0:T(8,128)(2,1)}) %all-gather.2.cloned.1.call-update) | async-done | bytes 1048592 | tf_op jit(solution)/shard_map/all_gather | solution.py:142
  125.4 2.7 %fusion.26 = f32[256,1024]{1,0:T(8,128)} fusion(bf16[512,1024]{1,0:T(8,128)(2,1)} %all-gather.2.cloned.1.call-done, f32[4,256,512]{2,1,0:T(8,128)S(1)} %copy-done.6, f32[256,512]{1,0:T(8,128)S(1)} %get-tuple-element.72, f32[512]{0:T(512)S(1)} %convert_element_type.80, f32[256]{0:T(256)S(1)} %get-tuple-element.82, f32[256]{0:T(256)S(1)} %get-tuple-element.81), kind=kOutput, calls=%fused_computation.50 | convolution fusion | flops 269090816 | bytes 3149824 | tf_op jit(solution)/shard_map/dot_general | solution.py:140
  128.2 19.5 %all-reduce.3.cloned.1.call-done = f32[256,1024]{1,0:T(8,128)} async-done(((f32[256,1024]{1,0:T(8,128)}), f32[256,1024]{1,0:T(8,128)}) %all-reduce.3.cloned.1.call-update) | async-done | bytes 1048592 | tf_op jit(solution)/shard_map/psum | solution.py:145
  147.7 1.6 multiply_reduce_fusion
  149.3 1.7 %fusion.31 = f32[1,256]{1,0:T(1,128)S(1)} fusion(bf16[256,1]{0,1:T(2,128)(2,1)S(1)} %reshape.187, bf16[1024,256]{1,0:T(8,128)(2,1)S(1)} %copy-done, f32[256,1024]{1,0:T(8,128)} %all-reduce.3.cloned.1.call-done, bf16[256,1024]{1,0:T(8,128)(2,1)S(1)} %bitcast.112, f32[1024]{0:T(1024)S(1)} %convert_element_type.82, f32[256]{0:T(256)S(1)} %add_rsqrt_fusion), kind=kOutput, calls=%fused_computation.55 | convolution fusion | flops 135987200 | bytes 2103808 | tf_op jit(solution)/shard_map/dot_general | solution.py:152
  151.2 0.7 fusion.39
  (58 shorter events, 1.2 us)
Async XLA Ops:
  6.5 142.8 %copy-start = (bf16[1024,256]{1,0:T(8,128)(2,1)S(1)}, bf16[1024,256]{1,0:T(8,128)(2,1)}, u32[]{:S(2)}) copy-start(bf16[1024,256]{1,0:T(8,128)(2,1)} %param.28) | copy-start | bytes 1572868
  6.5 48.9 %collective-permute-start = (bf16[4,512,512]{2,1,0:T(8,128)(2,1)}, bf16[4,512,512]{2,1,0:T(8,128)(2,1)}, u32[]{:S(2)}, u32[]{:S(2)}) collective-permute-start(bf16[4,512,512]{2,1,0:T(8,128)(2,1)} %param.24), channel_id=1, source_target_pairs={{0,2},{2,0},{1,3},{3,1},{4,6},{6,4},{5,7},{7,5},{8,10},{10,8},{9,1... | collective-permute-start | bytes 6291464 | tf_op jit(solution)/shard_map/ppermute | solution.py:63
  11.9 10.4 %all-to-all-start = ((s32[4,1,2]{2,1,0:T(1,128)}), s32[4,1,2]{2,1,0:T(1,128)S(1)}, u32[]{:S(2)}, u32[]{:S(2)}) async-start(s32[4,1,2]{2,1,0:T(1,128)} %bitcast.5), calls=%async_computation | async-start | bytes 4096 | tf_op jit(solution)/shard_map/all_to_all | solution.py:91
  16.7 38.7 %copy-start.7 = (bf16[4,64,1024]{2,1,0:T(8,128)(2,1)S(1)}, bf16[4,64,1024]{2,1,0:T(8,128)(2,1)}, u32[]{:S(2)}) copy-start(bf16[4,64,1024]{2,1,0:T(8,128)(2,1)} %param.18) | copy-start | bytes 1572868
  57.9 1.4 copy-start.5
  61.7 21.3 %copy-start.1 = (bf16[2,256,512]{2,1,0:T(8,128)(2,1)S(1)}, bf16[2,256,512]{2,1,0:T(8,128)(2,1)}, u32[]{:S(2)}) copy-start(bf16[2,256,512]{2,1,0:T(8,128)(2,1)} %param.23) | copy-start | bytes 1572868
  61.7 21.3 %copy-start.2 = (bf16[2,256,512]{2,1,0:T(8,128)(2,1)S(1)}, bf16[2,256,512]{2,1,0:T(8,128)(2,1)}, u32[]{:S(2)}) copy-start(bf16[2,256,512]{2,1,0:T(8,128)(2,1)} %param.22) | copy-start | bytes 1572868
  61.7 18.9 %all-to-all-start.1 = ((bf16[4,2,64,512]{3,2,1,0:T(8,128)(2,1)}), bf16[4,2,64,512]{3,2,1,0:T(8,128)(2,1)S(1)}, u32[]{:S(2)}, u32[]{:S(2)}) async-start(bf16[4,2,64,512]{3,2,1,0:T(8,128)(2,1)} %bitcast.25), calls=%async_computation.1 | async-start | bytes 1048576 | tf_op jit(solution)/shard_map/all_to_all | solution.py:90
  85.8 3.2 %copy-start.3 = (bf16[2,256,512]{2,1,0:T(8,128)(2,1)S(1)}, bf16[2,256,512]{2,1,0:T(8,128)(2,1)}, u32[]{:S(2)}) copy-start(bf16[2,256,512]{2,1,0:T(8,128)(2,1)} %get-tuple-element.183) | copy-start | bytes 1572868 | tf_op jit(solution)/shard_map/while
  89.1 6.9 %copy-start.10 = (s32[4,1]{0,1:T(1,128)S(1)}, s32[4,1]{0,1:T(1,128)}, u32[]{:S(2)}) copy-start(s32[4,1]{0,1:T(1,128)} %param.19) | copy-start | bytes 52
  89.1 7.1 %copy-start.11 = (bf16[512]{0:T(512)(128)(2,1)S(1)}, bf16[512]{0:T(512)(128)(2,1)}, u32[]{:S(2)}) copy-start(bf16[512]{0:T(512)(128)(2,1)} %param.25) | copy-start | bytes 3076
  89.1 7.1 %copy-start.4 = (f32[1,256,512]{2,1,0:T(8,128)S(1)}, f32[1,256,512]{2,1,0:T(8,128)}, u32[]{:S(2)}) copy-start(f32[1,256,512]{2,1,0:T(8,128)} %get-tuple-element.77) | copy-start | bytes 1572868
  91.7 17.5 %all-to-all-start.2 = ((bf16[4,2,64,512]{3,2,1,0:T(8,128)(2,1)}), bf16[4,2,64,512]{3,2,1,0:T(8,128)(2,1)S(1)}, u32[]{:S(2)}, u32[]{:S(2)}) async-start(bf16[4,2,64,512]{3,2,1,0:T(8,128)(2,1)} %bitcast.10), calls=%async_computation.2 | async-start | bytes 1048576 | tf_op jit(solution)/shard_map/all_to_all | solution.py:114
  95.1 30.2 %all-gather.2.cloned.1.call-start = ((), (), s32[]{:S(2)}) async-start(), calls=%async_computation.3 | async-start | bytes 1572864 | tf_op jit(solution)/shard_map/all_gather | solution.py:142
  95.9 51.9 %all-reduce.3.cloned.1.call-start = ((), (), s32[]{:S(2)}) async-start(), calls=%async_computation.4 | async-start | bytes 2097152 | tf_op jit(solution)/shard_map/psum | solution.py:145
  109.5 3.0 %copy-start.6 = (f32[4,256,512]{2,1,0:T(8,128)S(1)}, f32[4,256,512]{2,1,0:T(8,128)}, u32[]{:S(2)}) copy-start(f32[4,256,512]{2,1,0:T(8,128)} %copy-done.5) | copy-start | bytes 6291460
  125.4 2.8 %copy-start.9 = (bf16[1024]{0:T(1024)(128)(2,1)S(1)}, bf16[1024]{0:T(1024)(128)(2,1)}, u32[]{:S(2)}) copy-start(bf16[1024]{0:T(1024)(128)(2,1)} %param.27) | copy-start | bytes 6148
  125.4 2.8 %copy-start.13 = (bf16[256]{0:T(256)(128)(2,1)S(1)}, bf16[256]{0:T(256)(128)(2,1)}, u32[]{:S(2)}) copy-start(bf16[256]{0:T(256)(128)(2,1)} %param.29) | copy-start | bytes 1540
  128.1 21.2 %copy-start.8 = (bf16[4,64,1024]{2,1,0:T(8,128)(2,1)S(1)}, bf16[4,64,1024]{2,1,0:T(8,128)(2,1)}, u32[]{:S(2)}) copy-start(bf16[4,64,1024]{2,1,0:T(8,128)(2,1)} %param.18) | copy-start | bytes 1572868
  128.2 23.0 %copy-start.12 = (s32[4]{0:T(128)S(1)}, s32[4]{0:T(128)}, u32[]{:S(2)}) copy-start(s32[4]{0:T(128)} %param.21) | copy-start | bytes 52
Sparse Core Ops, SparseCore 0:
  97.5 27.8 all-gather.1
  128.3 19.4 all-reduce.2
